TPU v7x, 128 devices: a whole 4x4x4 slice. The times are simulated.
128 devices in a mesh: tp: 16 (over z, y), dp: 8 (over x, core).
Axes of the slice: x: 4, y: 4, z: 4, core: 2. Of those that a mesh axis runs over, the one named last changes fastest.
Arguments:
- feats: bfloat16 [2048, 36, 1024], P('dp')
- ln_gamma: float32 [1024], replicated
- ln_beta: float32 [1024], replicated
- w_head: bfloat16 [1024, 22528], P(None, 'tp')
- b_head: float32 [22528], P('tp')
- labels: int32 [2048], P('dp')
Outputs:
- output 1: float32 [], replicated
- output 2: bfloat16 [2048, 36, 1024], P('dp')
- output 3: float32 [1024, 22528], P(None, 'tp')
- output 4: float32 [22528], P('tp')
- output 5: float32 [1024], replicated
- output 6: float32 [1024], replicated
All inputs are finite; a program needn't handle non-finite values.
Results may differ from a plain program's by a relative error of at most 0.001.
Values sent between devices are 32-bit elements.
A program may use at most 1 GiB of HBM per device.

v0:
```python
import jax
import jax.numpy as jnp
from jax import lax
from jax.sharding import PartitionSpec as P

VALID_CLASSES = 21841
LN_EPS = 1e-5
SMOOTH = 0.1


def norm_pool(feats, ln_gamma, ln_beta):
    x_val = feats.astype(jnp.float32)
    mean_x = jnp.mean(x_val, axis=-1, keepdims=True)
    centered = x_val - mean_x
    var_x = jnp.mean(centered * centered, axis=-1, keepdims=True)
    inv_std = lax.rsqrt(var_x + LN_EPS)
    x_hat = centered * inv_std
    x_hat_mean = jnp.mean(x_hat, axis=1)
    pooled16 = (x_hat_mean * ln_gamma + ln_beta).astype(jnp.bfloat16)
    return x_hat, inv_std, x_hat_mean, pooled16


def norm_backward(grad_pool, x_hat, inv_std, x_hat_mean, ln_gamma):
    token_count = x_hat.shape[1]
    grad_gamma = jnp.sum(grad_pool * x_hat_mean, axis=0)
    grad_beta = jnp.sum(grad_pool, axis=0)
    upstream = grad_pool * ln_gamma / token_count
    up_mean = jnp.mean(upstream, axis=-1)
    proj_term = jnp.mean(x_hat * upstream[:, None, :], axis=-1, keepdims=True)
    grad_x = inv_std * (upstream[:, None, :] - up_mean[:, None, None] - x_hat * proj_term)
    return grad_x.astype(jnp.bfloat16), grad_gamma, grad_beta


def solution(mesh):
    data_size = mesh.shape["dp"]

    def local_head(feats, ln_gamma, ln_beta, w_head, b_head, labels):
        shard_cols = w_head.shape[1]
        global_rows = feats.shape[0] * data_size
        x_hat, inv_std, x_hat_mean, pooled16 = norm_pool(feats, ln_gamma, ln_beta)
        col_ids = lax.axis_index("tp") * shard_cols + jnp.arange(shard_cols)
        valid_mask = col_ids < VALID_CLASSES
        logits = jnp.dot(pooled16, w_head, preferred_element_type=jnp.float32) + b_head
        logits = jnp.where(valid_mask, logits, -1e30)
        row_max = lax.pmax(jnp.max(logits, axis=-1), "tp")
        shifted = jnp.exp(logits - row_max[:, None])
        onehot = col_ids == labels[:, None]
        row_stats = jnp.stack([jnp.sum(shifted, axis=-1), jnp.sum(jnp.where(onehot, logits, 0.0), axis=-1), jnp.sum(jnp.where(valid_mask, logits, 0.0), axis=-1)])
        row_stats = lax.psum(row_stats, "tp")
        log_norm = row_max + jnp.log(row_stats[0])
        loss_rows = log_norm - (1.0 - SMOOTH) * row_stats[1] - (SMOOTH / VALID_CLASSES) * row_stats[2]
        soft_probs = shifted / row_stats[0][:, None]
        dlogit = (soft_probs - (1.0 - SMOOTH) * onehot - (SMOOTH / VALID_CLASSES) * valid_mask) / global_rows
        dlogit16 = dlogit.astype(jnp.bfloat16)
        grad_w = lax.psum(lax.dot_general(pooled16, dlogit16, (((0,), (0,)), ((), ())), preferred_element_type=jnp.float32), "dp")
        grad_b = lax.psum(jnp.sum(dlogit, axis=0), "dp")
        grad_pool = lax.dot_general(dlogit16, w_head, (((1,), (1,)), ((), ())), preferred_element_type=jnp.float32)
        grad_pool = lax.psum(grad_pool, "tp")
        grad_feats, grad_gamma, grad_beta = norm_backward(grad_pool, x_hat, inv_std, x_hat_mean, ln_gamma)
        loss_sum, grad_gamma, grad_beta = lax.psum((jnp.sum(loss_rows), grad_gamma, grad_beta), "dp")
        return loss_sum / global_rows, grad_feats, grad_w, grad_b, grad_gamma, grad_beta

    return jax.shard_map(local_head, mesh=mesh, in_specs=(P("dp", None, None), P(), P(), P(None, "tp"), P("tp"), P("dp")), out_specs=(P(), P("dp", None, None), P(None, "tp"), P("tp"), P(), P()), check_vma=False)
```

profile of v0, /device:TPU:1, one launch (start us, length us, event | category | flops | bytes accessed | tf_op | source)
XLA Modules:
  0.0 298.8 jit_solution(97232354264421218)
XLA Ops:
  7.2 0.0 copy-start
  7.2 0.0 all-reduce.4.cloned.1.call-start
  7.3 0.8 broadcast_multiply_fusion.2
  8.1 7.7 %convert_reduce_fusion = f32[256,36]{0,1:T(8,128)S(1)} fusion(bf16[256,36,1024]{2,0,1:T(8,128)(2,1)} %param.6), kind=kLoop, calls=%fused_computation.1 | loop fusion | flops 18865152 | bytes 18911232 | tf_op jit(solution)/shard_map/reduce_sum | solution.py:13
  15.9 4.1 %copy-done.1 = bf16[256,36,1024]{2,0,1:T(8,128)(2,1)S(1)} copy-done((bf16[256,36,1024]{2,0,1:T(8,128)(2,1)S(1)}, bf16[256,36,1024]{2,0,1:T(8,128)(2,1)}, u32[]{:S(2)}) %copy-start.1) | copy-done | bytes 18874392
  20.0 6.3 %fusion.9 = f32[256,36]{0,1:T(8,128)S(1)} fusion(bf16[256,36,1024]{2,0,1:T(8,128)(2,1)S(1)} %copy-done.1, f32[256,36]{0,1:T(8,128)S(1)} %broadcast_multiply_fusion.1), kind=kLoop, calls=%fused_computation.11 | loop fusion | flops 37739520 | bytes 18948096 | tf_op jit(solution)/shard_map/reduce_sum | solution.py:15
  26.3 0.0 copy-start.4
  26.3 0.0 copy-start.7
  26.3 5.9 %fusion.4 = f32[256,1024]{1,0:T(8,128)S(1)} fusion(bf16[256,36,1024]{2,0,1:T(8,128)(2,1)S(1)} %copy-done.1, f32[256,36]{0,1:T(8,128)S(1)} %add_rsqrt_fusion, f32[256,36]{0,1:T(8,128)S(1)} %broadcast_multiply_fusion.1), kind=kLoop, calls=%fused_computation.6 | loop fusion | flops 37486592 | bytes 19996672 | tf_op jit(solution)/shard_map/reduce_sum | solution.py:18
  32.2 0.0 copy-done
  32.3 0.0 copy-start.6
  32.3 2.1 fusion.26
  34.4 35.5 %pmax.7 = f32[256]{0:T(256)S(1)} all-reduce(f32[256]{0:T(256)S(1)} %get-tuple-element.22), channel_id=1, replica_groups=mesh['tp'=16,'dp'=8] {'tp'}, use_global_device_ids=true, to_apply=%region_4.5 | all-reduce | flops 256 | bytes 2048 | tf_op jit(solution)/shard_map/pmax | solution.py:45
  69.9 1.9 fusion.15
  71.9 28.5 %psum.49 = f32[3,256]{1,0:T(4,128)S(1)} all-reduce(f32[3,256]{1,0:T(4,128)S(1)} %pad_maximum_fusion), channel_id=1, replica_groups=mesh['tp'=16,'dp'=8] {'tp'}, use_global_device_ids=true, to_apply=%region_8.9 | all-reduce | flops 768 | bytes 6144 | tf_op jit(solution)/shard_map/psum | solution.py:49
  100.4 3.6 %fusion.18 = f32[256,1024]{1,0:T(8,128)} fusion(bf16[1024,1408]{1,0:T(8,128)(2,1)S(1)} %copy-done, f32[256,1408]{1,0:T(8,128)} %get-tuple-element.23, f32[1408]{0:T(1024)S(1)} %broadcast_select_fusion, f32[256]{0:T(256)S(1)} %bitcast.8, s32[1408]{0:T(1024)S(1)} %iota_add_fusion, f32[256]{0:T(256)S(1)} %pmax.7, s32[256]{0:T(256)S(1)} %copy-done.6), kind=kOutput, calls=%fused_computation.29 | convolution fusion | flops 741081088 | bytes 5388288 | tf_op jit(solution)/shard_map/dot_general | solution.py:57
  103.9 0.0 all-reduce.4.cloned.1.call-update
  104.0 0.0 all-reduce.6.cloned.1.call-start
  104.0 5.6 %fusion.16 = f32[1024,1408]{1,0:T(8,128)} fusion(f32[256,1024]{1,0:T(8,128)} %copy-done.2, f32[1024]{0:T(1024)S(1)} %copy-done.4, f32[1024]{0:T(1024)S(1)} %broadcast_multiply_fusion.2, f32[256,1408]{1,0:T(8,128)} %get-tuple-element.23, f32[1408]{0:T(1024)S(1)} %broadcast_select_fusion, f32[256]{0:T(256)S(1)} %bitcast.9, s32[1408]{0:T(1024)S(1)} %iota_add_fusion, ...), kind=kOutput, calls=%fused_computation.27 | convolution fusion | flops 741867520 | bytes 8280064 | tf_op jit(solution)/shard_map/dot_general | solution.py:55
  109.6 0.0 all-reduce.6.cloned.1.call-update
  109.6 0.0 copy-start.5
  109.7 1.9 fusion.21
  111.6 0.6 subtract_reduce_fusion
  112.2 89.5 %all-reduce.4.cloned.1.call-done = f32[256,1024]{1,0:T(8,128)} async-done(((f32[256,1024]{1,0:T(8,128)}), f32[256,1024]{1,0:T(8,128)}) %all-reduce.4.cloned.1.call-update) | async-done | bytes 1048592 | tf_op jit(solution)/shard_map/psum | solution.py:58
  201.7 1.9 fusion.24
  203.6 13.3 %fusion.5 = f32[256,36]{0,1:T(8,128)S(1)} fusion(bf16[256,36,1024]{2,0,1:T(8,128)(2,1)} %param.6, f32[256,1024]{1,0:T(8,128)S(1)} %get-tuple-element.16, f32[256,36]{0,1:T(8,128)S(1)} %add_rsqrt_fusion, f32[256,36]{0,1:T(8,128)S(1)} %broadcast_multiply_fusion.1), kind=kLoop, calls=%fused_computation.7 | loop fusion | flops 47176704 | bytes 20033536 | tf_op jit(solution)/shard_map/reduce_sum | solution.py:29
  216.8 0.0 copy-done.3
  216.8 23.5 %all-reduce = (f32[]{:T(128)}, f32[1408]{0:T(1024)}, f32[1024]{0:T(1024)}, f32[1024]{0:T(1024)}) all-reduce(f32[]{:T(128)} %subtract_reduce_fusion, f32[1408]{0:T(1024)S(1)} %fusion.21, f32[1024]{0:T(1024)S(1)} %get-tuple-element.17, f32[1024]{0:T(1024)S(1)} %get-tuple-element.18), channel_id=1, replica_groups=mesh['tp'=16,'dp'=8] {'dp'}, use_global_device_ids=true, to_apply=%region_10.11 | all-reduce | flops 3457 | bytes 27656 | tf_op jit(solution)/shard_map/psum | solution.py:60
  241.1 1.4 broadcast_subtract_fusion
  242.4 20.4 %fusion.8 = bf16[256,36,1024]{2,0,1:T(8,128)(2,1)} fusion(bf16[256,36,1024]{2,0,1:T(8,128)(2,1)} %param.6, f32[256,36]{0,1:T(8,128)S(1)} %broadcast_multiply_fusion, f32[256,1024]{1,0:T(8,128)S(1)} %broadcast_subtract_fusion, f32[256,36]{0,1:T(8,128)S(1)} %add_rsqrt_fusion, f32[256,36]{0,1:T(8,128)S(1)} %broadcast_multiply_fusion.1), kind=kLoop, calls=%fused_computation.10 | loop fusion | flops 66060288 | bytes 38907904 | tf_op jit(solution)/shard_map/convert_element_type | solution.py:31
  262.8 22.4 %all-reduce.6.cloned.1.call-done = f32[1024,1408]{1,0:T(8,128)} async-done(((f32[1024,1408]{1,0:T(8,128)}), f32[1024,1408]{1,0:T(8,128)}) %all-reduce.6.cloned.1.call-update) | async-done | bytes 5767184 | tf_op jit(solution)/shard_map/psum | solution.py:55
  285.2 5.5 %copy.14 = f32[1024,1408]{1,0:T(8,128)} copy(f32[1024,1408]{1,0:T(8,128)} %all-reduce.6.cloned.1.call-done) | data formatting | bytes 11534336
  (17 shorter events, 0.1 us)
Async XLA Ops:
  7.2 25.1 %copy-start = (bf16[1024,1408]{1,0:T(8,128)(2,1)S(1)}, bf16[1024,1408]{1,0:T(8,128)(2,1)}, u32[]{:S(2)}) copy-start(bf16[1024,1408]{1,0:T(8,128)(2,1)} %param.9) | copy-start | bytes 8650756
  7.2 194.5 %all-reduce.4.cloned.1.call-start = ((), (), s32[]{:S(2)}) async-start(), calls=%async_computation | async-start | bytes 2097152 | tf_op jit(solution)/shard_map/psum | solution.py:58
  8.1 11.9 %copy-start.1 = (bf16[256,36,1024]{2,0,1:T(8,128)(2,1)S(1)}, bf16[256,36,1024]{2,0,1:T(8,128)(2,1)}, u32[]{:S(2)}) copy-start(bf16[256,36,1024]{2,0,1:T(8,128)(2,1)} %param.6) | copy-start | bytes 56623108
  26.3 6.0 %copy-start.4 = (f32[1024]{0:T(1024)S(1)}, f32[1024]{0:T(1024)}, u32[]{:S(2)}) copy-start(f32[1024]{0:T(1024)} %param.8) | copy-start | bytes 12292
  26.3 6.0 %copy-start.7 = (f32[1408]{0:T(1024)S(1)}, f32[1408]{0:T(1024)}, u32[]{:S(2)}) copy-start(f32[1408]{0:T(1024)} %param.10) | copy-start | bytes 16900
  32.3 2.1 copy-start.2
  32.3 37.6 %copy-start.6 = (s32[256]{0:T(256)S(1)}, s32[256]{0:T(256)}, u32[]{:S(2)}) copy-start(s32[256]{0:T(256)} %param.11) | copy-start | bytes 3076
  104.0 181.3 %all-reduce.6.cloned.1.call-start = ((), (), s32[]{:S(2)}) async-start(), calls=%async_computation.1 | async-start | bytes 11534336 | tf_op jit(solution)/shard_map/psum | solution.py:55
  109.6 92.0 %copy-start.5 = (f32[1024]{0:T(1024)S(1)}, f32[1024]{0:T(1024)}, u32[]{:S(2)}) copy-start(f32[1024]{0:T(1024)} %param.7) | copy-start | bytes 12292
  203.6 13.3 %copy-start.3 = (f32[256,1024]{1,0:T(8,128)}, f32[256,1024]{1,0:T(8,128)S(1)}, u32[]{:S(2)}) copy-start(f32[256,1024]{1,0:T(8,128)S(1)} %get-tuple-element.16) | copy-start | bytes 3145732
Sparse Core Ops, SparseCore 0:
  104.1 97.5 all-reduce.3
  204.6 80.5 all-reduce.5
where the time goes:
time: 299 us
  waiting for transfers between devices  112 us (37%)
  blocking collectives  87.6 us (29%)
  other arithmetic  62.2 us (21%)
  between operations  16 us (5%)
  matrix products  11.3 us (4%)
  local copies, waits for them, and re-layouts  9.68 us (3%)
    psum x1, waiting for transfers between devices, local_head(): grad_pool = lax.psum(grad_pool, 'tp')  89.5 us
    pmax x1, blocking collectives, local_head(): row_max = lax.pmax(jnp.max(logits, axis=-1), 'tp')  35.5 us
    psum x1, blocking collectives, local_head(): row_stats = lax.psum(row_stats, 'tp')  28.5 us
    psum x1, blocking collectives, local_head(): lax.psum((jnp.sum(loss_rows), grad_gamma, grad_beta), 'dp')  23.5 us
    psum x1, waiting for transfers between devices, local_head(): lax.psum(lax.dot_general(pooled16, dlogit16, (((0,), (0,)), ((), ())), pr...  22.4 us
    convert_element_type x1, other arithmetic, norm_backward(): return (grad_x.astype(jnp.bfloat16), grad_gamma, grad_beta)  20.4 us
    reduce_sum x1, other arithmetic, norm_backward(): proj_term = jnp.mean(x_hat * upstream[:, None, :], axis=-1, keepdims=True)  13.3 us
    unnamed x17, local copies, waits for them, and re-layouts  9.68 us
  transfers between devices with their start and end apart: 2, of which 2 were waited for; matrix products, arithmetic and copies ran while one was open for 15% of the time, Pallas kernels for 0%

commit v1 on v0

v1 whole, which is shorter than its diff:
```python
import functools

import jax
import jax.numpy as jnp
from jax import lax
from jax.experimental import pallas as pl
from jax.experimental.pallas import tpu as pltpu
from jax.sharding import PartitionSpec as P

VALID_CLASSES = 21841
LN_EPS = 1e-5
SMOOTH = 0.1
MESH = pl.DeviceIdType.MESH
F32 = jnp.float32
BF16 = jnp.bfloat16
LANES = 128
SIDES = {128: (4, 4, 4), 16: (2, 2, 2)}


def lane_ids(shape):
    return lax.broadcasted_iota(jnp.int32, shape, len(shape) - 1)


def head_kernel(
    sides, rows_total, f_ref, gam_ref, bet_ref, w_hbm, b_ref, lab_ref,
    loss_ref, dw_ref, db_ref, dg_ref, dbt_ref, dpool_ref, st_ref,
    fbuf, w, pf, p16, lg, dl16, dwbuf, dwrecv, xm, dpp, dpf, labs,
    ra, rb, ra2, rb2, ta, tb, sy, sz, gx, gc,
    f_sem, w_sem, x_send, x_recv, xl_send, xl_recv, g_send, g_recv, y_send, y_recv, z_send, z_recv,
    r_send, r_recv, d_send, d_recv, o_sem, q_send, q_recv,
):
    nx, ny, nz = sides
    npl = ny * nz
    tokens, ti, width = f_ref.shape
    cols = w.shape[1]
    half = ti // 2
    pb = half // npl
    ya, za = half // ny, half // nz
    tp, dp = lax.axis_index("tp"), lax.axis_index("dp")
    zi, yi = tp // ny, lax.rem(tp, ny)
    xi, ci = dp // 2, lax.rem(dp, 2)
    groups = ti // 8

    def dev(x=xi, y=yi, z=zi, c=ci):
        return {"tp": z * ny + y, "dp": x * 2 + c}

    xpeer = [(d, lax.rem(xi + d, nx)) for d in range(1, nx)]
    ypeer = [(d, lax.rem(yi + d, ny)) for d in range(1, ny)]
    zpeer = [(d, lax.rem(zi + d, nz)) for d in range(1, nz)]

    def remote(src, dst, ss, rs, who):
        return pltpu.make_async_remote_copy(src_ref=src, dst_ref=dst, send_sem=ss, recv_sem=rs, device_id=who, device_id_type=MESH)

    barrier = pltpu.get_barrier_semaphore()
    everyone = [dev(x=x) for _, x in xpeer] + [dev(y=y) for _, y in ypeer] + [dev(z=z) for _, z in zpeer] + [dev(c=1 - ci)]
    for who in everyone:
        pl.semaphore_signal(barrier, inc=1, device_id=who, device_id_type=MESH)

    ia, ib = zi * ny + yi, yi * nz + zi
    nslot = fbuf.shape[0]

    def arow(j):
        return pl.multiple_of(lax.rem(ia + j, npl) * pb, 8)

    def brow(j):
        return pl.multiple_of(half + lax.rem(ib + j, npl) * pb, 8)

    def fetch(j):
        slot = lax.rem(j, nslot)
        ca = pltpu.make_async_copy(f_ref.at[:, pl.ds(arow(j), pb), :], fbuf.at[slot, 0], f_sem.at[slot, 0])
        cb = pltpu.make_async_copy(f_ref.at[:, pl.ds(brow(j), pb), :], fbuf.at[slot, 1], f_sem.at[slot, 1])
        return ca, cb

    for j in range(nslot):
        for c in fetch(j):
            c.start()
    w_copy = pltpu.make_async_copy(w_hbm, w, w_sem)
    w_copy.start()
    labs[0] = lab_ref[...]
    st_ref[...] = jnp.zeros_like(st_ref)

    def norm_rows(slot, h, row0):
        x = fbuf[slot, h].astype(F32)
        mean = jnp.sum(x, axis=-1, keepdims=True) * (1.0 / width)
        cen = x - mean
        var = jnp.sum(cen * cen, axis=-1, keepdims=True) * (1.0 / width)
        inv = lax.rsqrt(var + LN_EPS)
        hat = jnp.sum(cen * inv, axis=0) * (1.0 / tokens)
        xm[pl.ds(row0, pb), :] = hat
        pf[0, pl.ds(row0, pb), :] = (hat * gam_ref[...] + bet_ref[...]).astype(BF16).astype(F32)
        blk = row0 // 8
        ids = lane_ids((tokens, 8, LANES))
        st_ref[...] = jnp.where(ids == blk, mean, jnp.where(ids == blk + 64, inv, st_ref[...]))

    def norm_chunk(j, prefetch):
        slot = lax.rem(j, nslot)
        for c in fetch(j):
            c.wait()

        def one(h, _):
            norm_rows(slot, h, pl.multiple_of(jnp.where(h == 0, arow(j), brow(j)), 8))
            return 0

        lax.fori_loop(0, 2, one, 0)
        if prefetch:
            for c in fetch(j + nslot):
                c.start()

    def norm_chunks(lo, hi):
        for a, b, pre in ((lo, min(hi, npl - nslot), True), (max(lo, npl - nslot), hi, False)):
            if b > a:
                lax.fori_loop(a, b, lambda j, _, pre=pre: (norm_chunk(j, pre), 0)[1], 0)

    sched = [1 * npl // 16, 5 * npl // 16, 10 * npl // 16]
    sched[0] = 1
    norm_chunks(0, 1)
    pl.semaphore_wait(barrier, len(everyone))

    own_a, own_b = pl.ds(arow(0), pb), pl.ds(brow(0), pb)
    xs = []
    for d, x in xpeer:
        for k, rows in enumerate((own_a, own_b)):
            xs.append(remote(pf.at[0, rows], pf.at[nx - d, rows], x_send.at[d - 1, k], x_recv.at[nx - d - 1, k], dev(x=x)))
        xs.append(remote(labs.at[0], labs.at[nx - d], xl_send.at[d - 1], xl_recv.at[nx - d - 1], dev(x=x)))
    for c in xs:
        c.start()
    norm_chunks(1, sched[1])
    for c in xs:
        c.wait()

    g1 = []
    for d, y in ypeer:
        g1.append(remote(pf.at[pl.ds(1, nx - 1), own_a], pf.at[pl.ds(1, nx - 1), own_a], g_send.at[0, d - 1], g_recv.at[0, ny - d - 1], dev(y=y)))
    for d, z in zpeer:
        g1.append(remote(pf.at[pl.ds(1, nx - 1), own_b], pf.at[pl.ds(1, nx - 1), own_b], g_send.at[1, d - 1], g_recv.at[1, nz - d - 1], dev(z=z)))
    for c in g1:
        c.start()
    norm_chunks(sched[1], sched[2])
    for c in g1:
        c.wait()
    blk_a = pl.ds(pl.multiple_of(zi * za, 8), za)
    blk_b = pl.ds(pl.multiple_of(half + yi * ya, 8), ya)
    g2 = []
    for d, z in zpeer:
        g2.append(remote(pf.at[pl.ds(1, nx - 1), blk_a], pf.at[pl.ds(1, nx - 1), blk_a], g_send.at[2, d - 1], g_recv.at[2, nz - d - 1], dev(z=z)))
    for d, y in ypeer:
        g2.append(remote(pf.at[pl.ds(1, nx - 1), blk_b], pf.at[pl.ds(1, nx - 1), blk_b], g_send.at[3, d - 1], g_recv.at[3, ny - d - 1], dev(y=y)))
    for c in g2:
        c.start()
    norm_chunks(sched[2], npl)
    w_copy.wait()

    col = (tp * cols + lane_ids((1, cols))).astype(F32)
    valid = col < float(VALID_CLASSES)
    vweight = jnp.where(valid, SMOOTH / VALID_CLASSES, 0.0)
    sub = 32
    lane8 = lane_ids((8, LANES))

    def col_of(packed, lane):
        return jnp.sum(jnp.where(lane8 == lane, packed, 0.0), axis=-1, keepdims=True)

    def label_col(slot, r):
        return jnp.concatenate([col_of(labs[slot], r * (sub // 8) + k) for k in range(sub // 8)], axis=0)

    sy[yi] = jnp.zeros_like(sy[0])

    def logits_of(slot):
        xabs = lax.rem(xi + slot, nx)
        p16[xabs] = pf[slot].astype(BF16)
        lg[xabs] = jnp.dot(p16[xabs], w[...], preferred_element_type=F32)

        def body(r, _):
            rows = pl.ds(pl.multiple_of(r * sub, sub), sub)
            l = jnp.where(valid, lg[xabs, rows, :] + b_ref[...], -1e30)
            m = jnp.max(l, axis=-1, keepdims=True)
            e = jnp.exp(l - m)
            s = jnp.sum(e, axis=-1, keepdims=True)
            lg[xabs, rows, :] = e
            hot = col == label_col(slot, r)
            part = jnp.where(hot, (1.0 - SMOOTH) * l, 0.0) + vweight * l
            ps = jnp.sum(part, axis=-1, keepdims=True)
            ms, ss, pp = sy[yi, 0], sy[yi, 1], sy[yi, 2]
            for k in range(sub // 8):
                here = lane8 == xabs * groups + r * (sub // 8) + k
                ms = jnp.where(here, m[8 * k : 8 * k + 8], ms)
                ss = jnp.where(here, s[8 * k : 8 * k + 8], ss)
                pp = jnp.where(here, ps[8 * k : 8 * k + 8], pp)
            sy[yi, 0], sy[yi, 1], sy[yi, 2] = ms, ss, pp
            return 0

        lax.fori_loop(0, ti // sub, body, 0)

    logits_of(0)
    for c in g2:
        c.wait()
    lax.fori_loop(1, nx, lambda s, _: (logits_of(s), 0)[1], 0)
    mine_m = sy[yi, 0]

    st1 = [remote(sy.at[yi], sy.at[yi], y_send.at[d - 1], y_recv.at[ny - d - 1], dev(y=y)) for d, y in ypeer]
    for c in st1:
        c.start()
    for c in st1:
        c.wait()

    def merge(buf, n):
        m = buf[0, 0]
        for k in range(1, n):
            m = jnp.maximum(m, buf[k, 0])
        s = jnp.zeros_like(m)
        q = jnp.zeros_like(m)
        for k in range(n):
            s = s + buf[k, 1] * jnp.exp(buf[k, 0] - m)
            q = q + buf[k, 2]
        return m, s, q

    m, s, q = merge(sy, ny)
    sz[zi, 0], sz[zi, 1], sz[zi, 2] = m, s, q
    st2 = [remote(sz.at[zi], sz.at[zi], z_send.at[d - 1], z_recv.at[nz - d - 1], dev(z=z)) for d, z in zpeer]
    for c in st2:
        c.start()
    for c in st2:
        c.wait()
    m, s, q = merge(sz, nz)
    used = lane8 < nx * groups
    coef = jnp.where(used, jnp.exp(mine_m - m) / s * (1.0 / rows_total), 0.0)
    loss_rows = jnp.where(used, m + jnp.log(jnp.where(used, s, 1.0)) - q, 0.0)
    sz[zi, 0] = coef
    vscaled = vweight * (1.0 / rows_total)
    hotscaled = (1.0 - SMOOTH) / rows_total

    def dlogit_of(slot, acc):
        xabs = lax.rem(xi + slot, nx)

        def body(r, acc):
            rows = pl.ds(pl.multiple_of(r * sub, sub), sub)
            cc = sz[zi, 0]
            cf = jnp.concatenate([col_of(cc, xabs * groups + r * (sub // 8) + k) for k in range(sub // 8)], axis=0)
            hot = col == label_col(slot, r)
            dl = lg[xabs, rows, :] * cf - jnp.where(hot, hotscaled, 0.0) - vscaled
            dl16[xabs, rows, :] = dl.astype(BF16)
            lg[xabs, rows, :] = dl
            return acc

        return lax.fori_loop(0, ti // sub, body, acc)

    dlogit_of(0, 0)
    dpp[...] = lax.dot_general(dl16[xi], w[...], (((1,), (1,)), ((), ())), preferred_element_type=F32)

    r1 = []
    for d, z in zpeer:
        r1.append(remote(dpp.at[pl.ds(pl.multiple_of(z * za, 8), za)], ra.at[nz - d - 1], r_send.at[0, d - 1], r_recv.at[0, nz - d - 1], dev(z=z)))
    for d, y in ypeer:
        r1.append(remote(dpp.at[pl.ds(pl.multiple_of(half + y * ya, 8), ya)], rb.at[ny - d - 1], r_send.at[1, d - 1], r_recv.at[1, ny - d - 1], dev(y=y)))
    for c in r1:
        c.start()
    lax.fori_loop(1, nx, lambda s, a: dlogit_of(s, a), 0)

    def dbody(r, acc):
        return acc + lg[r // groups, pl.ds(pl.multiple_of(lax.rem(r, groups) * 8, 8), 8), :]

    db8 = lax.fori_loop(0, nx * groups, dbody, jnp.zeros((8, cols), F32))
    db_mine = jnp.sum(db8, axis=0, keepdims=True)
    for c in r1:
        c.wait()

    def total(buf, own, n):
        t = own
        for k in range(n - 1):
            t = t + buf[k]
        return t

    ta[...] = total(ra, dpp[blk_a, :], nz)
    tb[...] = total(rb, dpp[blk_b, :], ny)
    r2 = []
    for d, y in ypeer:
        r2.append(remote(ta.at[pl.ds(pl.multiple_of(y * pb, 8), pb)], ra2.at[ny - d - 1], r_send.at[2, d - 1], r_recv.at[2, ny - d - 1], dev(y=y)))
    for d, z in zpeer:
        r2.append(remote(tb.at[pl.ds(pl.multiple_of(z * pb, 8), pb)], rb2.at[nz - d - 1], r_send.at[3, d - 1], r_recv.at[3, nz - d - 1], dev(z=z)))
    for c in r2:
        c.start()

    mh = width // 2

    def dw_half(h):
        lhs_cols = pl.ds(pl.multiple_of(h * mh, 128), mh)
        k = nx * ti
        dwbuf[h] = lax.dot_general(p16[:, :, lhs_cols].reshape(k, mh), dl16[...].reshape(k, cols), (((0,), (0,)), ((), ())), preferred_element_type=F32)

    dw_half(1 - ci)
    ex = remote(dwbuf.at[1 - ci], dwrecv, d_send.at[0], d_recv.at[0], dev(c=1 - ci))
    ex.start()
    for c in r2:
        c.wait()
    dpf[own_a, :] = total(ra2, ta[pl.ds(pl.multiple_of(yi * pb, 8), pb), :], ny)
    dpf[own_b, :] = total(rb2, tb[pl.ds(pl.multiple_of(zi * pb, 8), pb), :], nz)
    a1 = []
    for d, y in ypeer:
        a1.append(remote(dpf.at[own_a], dpf.at[own_a], r_send.at[4, d - 1], r_recv.at[4, ny - d - 1], dev(y=y)))
    for d, z in zpeer:
        a1.append(remote(dpf.at[own_b], dpf.at[own_b], r_send.at[5, d - 1], r_recv.at[5, nz - d - 1], dev(z=z)))
    for c in a1:
        c.start()
    dw_half(ci)
    for c in a1:
        c.wait()
    a2 = []
    for d, z in zpeer:
        a2.append(remote(dpf.at[blk_a], dpf.at[blk_a], r_send.at[6, d - 1], r_recv.at[6, nz - d - 1], dev(z=z)))
    for d, y in ypeer:
        a2.append(remote(dpf.at[blk_b], dpf.at[blk_b], r_send.at[7, d - 1], r_recv.at[7, ny - d - 1], dev(y=y)))
    for c in a2:
        c.start()
    ex.wait()
    dwbuf[ci] = dwbuf[ci] + dwrecv[...]
    out_rows = pl.ds(pl.multiple_of(ci * mh, 8), mh)
    o_local = pltpu.make_async_copy(dwbuf.at[ci], dw_ref.at[out_rows], o_sem)
    o_far = remote(dwbuf.at[ci], dw_ref.at[out_rows], d_send.at[1], d_recv.at[1], dev(c=1 - ci))
    o_local.start()
    o_far.start()
    for c in a2:
        c.wait()
    dpool_ref[...] = dpf[...]

    gx[xi, 0:1, :] = jnp.sum(dpf[...] * xm[...], axis=0, keepdims=True)
    gx[xi, 1:2, :] = jnp.sum(dpf[...], axis=0, keepdims=True)
    t1 = [remote(gx.at[xi], gx.at[xi], q_send.at[d - 1], q_recv.at[nx - d - 1], dev(x=x)) for d, x in xpeer]
    for c in t1:
        c.start()
    for c in t1:
        c.wait()
    tot = gx[0]
    for k in range(1, nx):
        tot = tot + gx[k]
    gc[0, :, 0:width] = tot
    gc[0, 0:1, width : width + cols] = db_mine
    gc[0, :, width + cols :] = loss_rows
    t2 = remote(gc.at[0], gc.at[1], q_send.at[nx - 1], q_recv.at[nx - 1], dev(c=1 - ci))
    t2.start()
    t2.wait()
    both = gc[0] + gc[1]
    dg_ref[...] = both[0:1, 0:width]
    dbt_ref[...] = both[1:2, 0:width]
    db_ref[...] = both[0:1, width : width + cols]
    lsum = jnp.sum(jnp.sum(both[:, width + cols :], axis=-1, keepdims=True), axis=0, keepdims=True)
    loss_ref[...] = jnp.broadcast_to(lsum * (1.0 / rows_total), loss_ref.shape)
    o_local.wait()
    o_far.wait()


def norm_bwd_kernel(blocks, f_ref, dp_ref, gam_ref, st_ref, out_ref):
    tokens, rows, width = f_ref.shape
    i = pl.program_id(0)
    ids = lane_ids((tokens, 8, LANES))

    def one(h, _):
        r = pl.ds(pl.multiple_of(h * 8, 8), 8)
        blk = i * (rows // 8) + h
        u = dp_ref[r, :] * gam_ref[...] * (1.0 / tokens)
        ut = u - jnp.mean(u, axis=-1, keepdims=True)
        st = st_ref[...]
        mean = jnp.sum(jnp.where(ids == blk, st, 0.0), axis=-1, keepdims=True)
        inv = jnp.sum(jnp.where(ids == blk + 64, st, 0.0), axis=-1, keepdims=True)
        cen = f_ref[:, r, :].astype(F32) - mean
        proj = jnp.sum(cen * ut[None], axis=-1, keepdims=True) * inv * (1.0 / width)
        out_ref[:, r, :] = (inv * (ut[None] - cen * (inv * proj))).astype(BF16)
        return 0

    lax.fori_loop(0, rows // 8, one, 0)


def solution(mesh):
    sides = SIDES[mesh.devices.size]
    nx, ny, nz = sides
    dp_size = mesh.shape["dp"]

    def local_head(feats, ln_gamma, ln_beta, w_head, b_head, labels):
        ti, tokens, width = feats.shape
        cols = w_head.shape[1]
        half = ti // 2
        pb = half // (ny * nz)
        ft = jnp.transpose(feats, (1, 0, 2))
        gam, bet, bias = ln_gamma[None], ln_beta[None], b_head[None]
        lab = jnp.pad(labels.astype(F32).reshape(ti // 8, 8).T, ((0, 0), (0, LANES - ti // 8)))
        vm = pl.BlockSpec(memory_space=pltpu.VMEM)
        hbm = pl.BlockSpec(memory_space=pl.ANY)
        sem = pltpu.SemaphoreType.DMA
        n3 = max(nx, ny, nz)
        S = jax.ShapeDtypeStruct
        loss, dw, db, dg, dbt, dpool, st = pl.pallas_call(
            functools.partial(head_kernel, sides, ti * dp_size),
            out_shape=(S((8, LANES), F32), S((width, cols), F32), S((1, cols), F32), S((1, width), F32), S((1, width), F32), S((ti, width), F32), S((tokens, 8, LANES), F32)),
            in_specs=[hbm, vm, vm, hbm, vm, vm],
            out_specs=(vm, hbm, vm, vm, vm, vm, vm),
            scratch_shapes=[
                pltpu.VMEM((min(4, ny * nz), 2, tokens, pb, width), BF16),
                pltpu.VMEM((width, cols), BF16),
                pltpu.VMEM((nx, ti, width), F32),
                pltpu.VMEM((nx, ti, width), BF16),
                pltpu.VMEM((nx, ti, cols), F32),
                pltpu.VMEM((nx, ti, cols), BF16),
                pltpu.VMEM((2, width // 2, cols), F32),
                pltpu.VMEM((width // 2, cols), F32),
                pltpu.VMEM((ti, width), F32),
                pltpu.VMEM((ti, width), F32),
                pltpu.VMEM((ti, width), F32),
                pltpu.VMEM((nx, 8, LANES), F32),
                pltpu.VMEM((nz - 1, half // nz, width), F32),
                pltpu.VMEM((ny - 1, half // ny, width), F32),
                pltpu.VMEM((ny - 1, pb, width), F32),
                pltpu.VMEM((nz - 1, pb, width), F32),
                pltpu.VMEM((half // nz, width), F32),
                pltpu.VMEM((half // ny, width), F32),
                pltpu.VMEM((ny, 3, 8, LANES), F32),
                pltpu.VMEM((nz, 3, 8, LANES), F32),
                pltpu.VMEM((nx, 8, width), F32),
                pltpu.VMEM((2, 8, width + cols + LANES), F32),
                sem((min(4, ny * nz), 2)),
                sem,
                sem((nx - 1, 2)), sem((nx - 1, 2)), sem((nx - 1,)), sem((nx - 1,)),
                sem((4, n3 - 1)), sem((4, n3 - 1)),
                sem((ny - 1,)), sem((ny - 1,)), sem((nz - 1,)), sem((nz - 1,)),
                sem((8, n3 - 1)), sem((8, n3 - 1)),
                sem((2,)), sem((2,)), sem,
                sem((nx,)), sem((nx,)),
            ],
            compiler_params=pltpu.CompilerParams(collective_id=0, has_side_effects=True, vmem_limit_bytes=60 * 1024 * 1024),
        )(ft, gam, bet, w_head, bias, lab)
        rb = 16
        dft = pl.pallas_call(
            functools.partial(norm_bwd_kernel, ti // 8),
            grid=(ti // rb,),
            out_shape=S((tokens, ti, width), BF16),
            in_specs=[
                pl.BlockSpec((tokens, rb, width), lambda i: (0, i, 0)),
                pl.BlockSpec((rb, width), lambda i: (i, 0)),
                pl.BlockSpec((1, width), lambda i: (0, 0)),
                pl.BlockSpec((tokens, 8, LANES), lambda i: (0, 0, 0)),
            ],
            out_specs=pl.BlockSpec((tokens, rb, width), lambda i: (0, i, 0)),
            compiler_params=pltpu.CompilerParams(vmem_limit_bytes=40 * 1024 * 1024),
        )(ft, dpool, gam, st)
        return loss[0, 0], jnp.transpose(dft, (1, 0, 2)), dw, db[0], dg[0], dbt[0]

    return jax.shard_map(
        local_head,
        mesh=mesh,
        in_specs=(P("dp", None, None), P(), P(), P(None, "tp"), P("tp"), P("dp")),
        out_specs=(P(), P("dp", None, None), P(None, "tp"), P("tp"), P(), P()),
        check_vma=False,
    )
```

time: 299 us -> 123 us (0.41)
  waiting for transfers between devices: 112 us -> 0 us
  Pallas kernels: 0 us -> 111 us
  blocking collectives: 87.6 us -> 0 us
  other arithmetic: 62.2 us -> 1.99 us
  between operations: 16 us -> 0.65 us
  matrix products: 11.3 us -> 0 us
    psum x2 -> x0, waiting for transfers between devices: 112 us -> none  [the longest x1 89.5 us: local_head(): grad_pool = lax.psum(grad_pool, 'tp')]
    pallas_call x0 -> x2, Pallas kernels: none -> 111 us  [the longest x1 88.1 us: local_head(): pl.pallas_call(functools.partial(head_kernel, sides, ti * dp_size), out_s...]
    psum x2 -> x0, blocking collectives: 52.1 us -> none  [the longest x1 28.5 us: local_head(): row_stats = lax.psum(row_stats, 'tp')]
    reduce_sum x8 -> x0, other arithmetic: 39.6 us -> none  [the longest x1 13.3 us: norm_backward(): proj_term = jnp.mean(x_hat * upstream[:, None, :], axis=-1, keepdims=True)]
    pmax x1 -> x0, blocking collectives: 35.5 us -> none  [local_head(): row_max = lax.pmax(jnp.max(logits, axis=-1), 'tp')]
    convert_element_type x1, other arithmetic: 20.4 us -> 0.68 us  [local_head(): labels.astype(F32).reshape(ti // 8, 8)]
    dot_general x3 -> x0, matrix products: 11.3 us -> none  [the longest x1 5.61 us: local_head(): lax.dot_general(pooled16, dlogit16, (((0,), (0,)), ((), ())), preferred_e...]
    unnamed x17 -> x15, local copies, waits for them, and re-layouts: 9.68 us -> 5.87 us
  transfers between devices with their start and end apart: 2 -> 0, of which waited for: 2 -> 0; matrix products, arithmetic and copies ran while one was open for 15% -> 0% of each run, Pallas kernels for 0% -> 0%
where the time goes in v1:
time: 123 us; the launch traced here: 122 us
  Pallas kernels  111 us (90%)
  local copies, waits for them, and re-layouts  9.12 us (7%)
  other arithmetic  1.99 us (2%)
    pallas_call x1, Pallas kernels, local_head(): pl.pallas_call(functools.partial(head_kernel, sides, ti * dp_size), out_s...  88.1 us
    pallas_call x1, Pallas kernels, local_head(): pl.pallas_call(functools.partial(norm_bwd_kernel, ti // 8), grid=(ti // r...  22.6 us
    unnamed x15, local copies, waits for them, and re-layouts  5.87 us

profile of v1, /device:TPU:1, one launch (start us, length us, event | category | flops | bytes accessed | tf_op | source)
XLA Modules:
  0.0 122.5 jit_solution(1012444682518044732)
XLA Ops:
  0.6 0.7 convert_element_type.5
  1.3 1.3 %broadcast_in_dim.11.b_ref = f32[1,1408]{1,0:T(1,128)} reshape(f32[1408]{0:T(1024)} %param.10) | data formatting | bytes 11264 | tf_op jit(solution)/shard_map/broadcast_in_dim | solution.py:382
  2.6 0.1 reshape.15
  2.7 0.1 copy.12
  2.8 0.6 pad.4.lab_ref
  3.4 0.0 copy-start.2
  3.4 88.1 %shard_map.109 = (f32[8,128]{1,0:T(8,128)}, f32[1024,1408]{1,0:T(8,128)}, f32[1,1408]{1,0:T(1,128)}, f32[1,1024]{1,0:T(1,128)}, f32[1,1024]{1,0:T(1,128)}, /*index=5*/f32[256,1024]{1,0:T(8,128)}, f32[36,8,128]{2,1,0:T(8,128)}) custom-call(bf16[36,256,1024]{2,1,0:T(8,128)(2,1)} %bitcast.10, f32[1,1024]{1,0:T(1,128)} %bitcast.8, f32[1,1024]{1,0:T(1,128)} %bitcast.16, ...), custom_call_target="tpu_custom_call" | custom-call | tf_op jit(solution)/shard_map/pallas_call | solution.py:389
  91.5 1.2 slice.3
  92.7 1.3 %reduce = f32[1408]{0:T(1024)} reduce(f32[1,1408]{1,0:T(1,128)} %get-tuple-element.17, f32[]{:T(128)} %constant.5), dimensions={0}, to_apply=%get-tuple-element.17.reduce_sub_computation | reduce | bytes 11268 | tf_op jit(solution)/shard_map/pallas_call | solution.py:389
  94.0 0.0 copy-done.2
  94.0 0.0 copy-start
  94.0 1.2 copy-done
  95.2 0.0 copy-start.1
  95.2 0.9 copy-done.1
  96.1 0.0 copy-start.3
  96.1 22.6 %shard_map.110 = bf16[36,256,1024]{2,1,0:T(8,128)(2,1)} custom-call(bf16[36,256,1024]{2,1,0:T(8,128)(2,1)} %bitcast.11, f32[256,1024]{1,0:T(8,128)S(1)} %copy-done, f32[1,1024]{1,0:T(1,128)S(1)} %bitcast.9, f32[36,8,128]{2,1,0:T(8,128)S(1)} %copy-done.1), custom_call_target="tpu_custom_call" | custom-call | tf_op jit(solution)/shard_map/pallas_call | solution.py:429
  118.7 0.0 copy-done.3
  118.7 0.0 copy-start.5
  118.7 0.0 copy-start.4
  118.7 2.5 %copy.16 = f32[1024,1408]{1,0:T(8,128)} copy(f32[1024,1408]{1,0:T(8,128)S(1)} %copy-done.3) | data formatting | bytes 11534336
  121.3 0.0 copy-done.5
  121.3 0.6 copy.17
  121.9 0.0 copy-done.4
  121.9 0.6 copy.18
Async XLA Ops:
  3.4 90.6 %copy-start.2 = (f32[1024]{0:T(1024)S(1)}, f32[1024]{0:T(1024)}, u32[]{:S(2)}) copy-start(f32[1024]{0:T(1024)} %param.7) | copy-start | bytes 12292
  94.0 1.2 %copy-start = (f32[256,1024]{1,0:T(8,128)S(1)}, f32[256,1024]{1,0:T(8,128)}, u32[]{:S(2)}) copy-start(f32[256,1024]{1,0:T(8,128)} %get-tuple-element.14.dp_ref) | copy-start | bytes 3145732
  95.2 0.9 copy-start.1
  96.1 22.6 %copy-start.3 = (f32[1024,1408]{1,0:T(8,128)S(1)}, f32[1024,1408]{1,0:T(8,128)}, u32[]{:S(2)}) copy-start(f32[1024,1408]{1,0:T(8,128)} %get-tuple-element.28) | copy-start | bytes 17301508
  118.7 2.5 %copy-start.5 = (f32[1,1024]{1,0:T(1,128)S(1)}, f32[1,1024]{1,0:T(1,128)}, u32[]{:S(2)}) copy-start(f32[1,1024]{1,0:T(1,128)} %get-tuple-element.18) | copy-start | bytes 12292
  118.7 3.1 %copy-start.4 = (f32[1,1024]{1,0:T(1,128)S(1)}, f32[1,1024]{1,0:T(1,128)}, u32[]{:S(2)}) copy-start(f32[1,1024]{1,0:T(1,128)} %get-tuple-element.19) | copy-start | bytes 12292

commit v2 on v1

v2 whole, which is shorter than its diff:
```python
import functools

import jax
import jax.numpy as jnp
from jax import lax
from jax.experimental import pallas as pl
from jax.experimental.pallas import tpu as pltpu
from jax.sharding import PartitionSpec as P

VALID_CLASSES = 21841
LN_EPS = 1e-5
SMOOTH = 0.1
MESH = pl.DeviceIdType.MESH
F32 = jnp.float32
BF16 = jnp.bfloat16
LANES = 128
SIDES = {128: (4, 4, 4), 16: (2, 2, 2)}


def lane_ids(shape):
    return lax.broadcasted_iota(jnp.int32, shape, len(shape) - 1)


def head_kernel(
    sides, rows_total, f_ref, gam_ref, bet_ref, w_hbm, b_ref, lab_ref,
    dwbuf, small_ref, dpf, st_ref,
    fbuf, w, pf, p16, lg, dl16, dwpart, dwrecv, xm, dpp, labs,
    ra, rb, ra2, rb2, ta, tb, stat, cof, gy, gz, gx, gc,
    f_sem, w_sem, x_send, x_recv, xl_send, xl_recv, xd_send, xd_recv, g_send, g_recv, s_send, s_recv,
    r_send, r_recv, d_send, d_recv, q_send, q_recv,
):
    nx, ny, nz = sides
    npl = ny * nz
    tokens, ti, width = f_ref.shape
    cols = w.shape[1]
    direct = width * 3 // 8
    half = ti // 2
    pb = half // npl
    ya, za = half // ny, half // nz
    tp, dp = lax.axis_index("tp"), lax.axis_index("dp")
    zi, yi = tp // ny, lax.rem(tp, ny)
    xi, ci = dp // 2, lax.rem(dp, 2)
    groups = ti // 8

    def dev(x=xi, y=yi, z=zi, c=ci):
        return {"tp": z * ny + y, "dp": x * 2 + c}

    xpeer = [(d, lax.rem(xi + d, nx)) for d in range(1, nx)]
    ypeer = [(d, lax.rem(yi + d, ny)) for d in range(1, ny)]
    zpeer = [(d, lax.rem(zi + d, nz)) for d in range(1, nz)]

    def remote(src, dst, ss, rs, who):
        return pltpu.make_async_remote_copy(src_ref=src, dst_ref=dst, send_sem=ss, recv_sem=rs, device_id=who, device_id_type=MESH)

    barrier = pltpu.get_barrier_semaphore()
    plane = [(dz * ny + dy, dev(y=lax.rem(yi + dy, ny), z=lax.rem(zi + dz, nz))) for dz in range(nz) for dy in range(ny) if dz or dy]
    everyone = [dev(x=x) for _, x in xpeer] + [who for _, who in plane] + [dev(c=1 - ci)]
    for who in everyone:
        pl.semaphore_signal(barrier, inc=1, device_id=who, device_id_type=MESH)

    ia, ib = zi * ny + yi, yi * nz + zi
    nslot = fbuf.shape[0]

    def arow(j):
        return pl.multiple_of(lax.rem(ia + j, npl) * pb, 8)

    def brow(j):
        return pl.multiple_of(half + lax.rem(ib + j, npl) * pb, 8)

    def fetch(j):
        slot = lax.rem(j, nslot)
        ca = pltpu.make_async_copy(f_ref.at[:, pl.ds(arow(j), pb), :], fbuf.at[slot, 0], f_sem.at[slot, 0])
        cb = pltpu.make_async_copy(f_ref.at[:, pl.ds(brow(j), pb), :], fbuf.at[slot, 1], f_sem.at[slot, 1])
        return ca, cb

    for j in range(nslot):
        for c in fetch(j):
            c.start()
    w_copy = pltpu.make_async_copy(w_hbm, w, w_sem)
    w_copy.start()
    st_ref[...] = jnp.zeros_like(st_ref)
    lane8 = lane_ids((8, LANES))
    row8 = lax.broadcasted_iota(jnp.int32, (8, LANES), 0)

    def norm_rows(slot, h, row0):
        x = fbuf[slot, h].astype(F32)
        mean = jnp.sum(x, axis=-1, keepdims=True) * (1.0 / width)
        cen = x - mean
        var = jnp.sum(cen * cen, axis=-1, keepdims=True) * (1.0 / width)
        inv = lax.rsqrt(var + LN_EPS)
        hat = jnp.sum(cen * inv, axis=0) * (1.0 / tokens)
        xm[pl.ds(row0, pb), :] = hat
        pf[0, pl.ds(row0, pb), :] = (hat * gam_ref[...] + bet_ref[...]).astype(BF16).astype(F32)
        blk = row0 // 8
        ids = lane_ids((tokens, 8, LANES))
        st_ref[...] = jnp.where(ids == blk, mean, jnp.where(ids == blk + 64, inv, st_ref[...]))

    def norm_chunk(j, prefetch):
        slot = lax.rem(j, nslot)
        for c in fetch(j):
            c.wait()

        def one(h, _):
            norm_rows(slot, h, pl.multiple_of(jnp.where(h == 0, arow(j), brow(j)), 8))
            return 0

        lax.fori_loop(0, 2, one, 0)
        if prefetch:
            for c in fetch(j + nslot):
                c.start()

    def norm_chunks(lo, hi):
        for a, b, pre in ((lo, min(hi, npl - nslot), True), (max(lo, npl - nslot), hi, False)):
            if b > a:
                lax.fori_loop(a, b, lambda j, _, pre=pre: (norm_chunk(j, pre), 0)[1], 0)

    dcols, pcols = pl.ds(0, direct), pl.ds(direct, width - direct)

    def straight(j):
        out = []
        for d, x in xpeer:
            for rows in (arow(j), brow(j)):
                rows = pl.ds(rows, pb)
                out.append(remote(pf.at[0, rows, dcols], pf.at[nx - d, rows, dcols], xd_send.at[d - 1], xd_recv.at[nx - d - 1], dev(x=x)))
        return out

    def send_straight(j):
        for c in straight(j):
            c.start()

    def norm_and_send(lo, hi):
        for a, b, pre in ((lo, min(hi, npl - nslot), True), (max(lo, npl - nslot), hi, False)):
            if b > a:
                lax.fori_loop(a, b, lambda j, _, pre=pre: (norm_chunk(j, pre), send_straight(j), 0)[2], 0)

    first = min(3, npl // 2)
    cuts = [first, npl // 2, npl * 13 // 16]
    norm_chunks(0, first)

    def pack_labels(g, acc):
        for k in range(8):
            acc = jnp.where((lane8 == g) & (row8 == k), lab_ref[g * 8 + k].astype(F32), acc)
        return acc

    labs[0] = lax.fori_loop(0, groups, pack_labels, jnp.zeros((8, LANES), F32))
    pl.semaphore_wait(barrier, len(everyone))

    own_a, own_b = pl.ds(arow(0), pb), pl.ds(brow(0), pb)
    order = sorted(range(1, nx), key=lambda slot: min(slot, nx - slot))
    xs = {}
    for d, x in sorted(xpeer, key=lambda dx: min(dx[0], nx - dx[0])):
        xs[nx - d] = []
        for k, rows in enumerate((own_a, own_b)):
            xs[nx - d].append(remote(pf.at[0, rows, pcols], pf.at[nx - d, rows, pcols], x_send.at[nx - d - 1, k], x_recv.at[nx - d - 1, k], dev(x=x)))
        xs[nx - d].append(remote(labs.at[0], labs.at[nx - d], xl_send.at[nx - d - 1], xl_recv.at[nx - d - 1], dev(x=x)))
        for c in xs[nx - d]:
            c.start()
    lax.fori_loop(0, first, lambda j, _: (send_straight(j), 0)[1], 0)
    norm_and_send(first, cuts[1])

    blk_a = pl.ds(pl.multiple_of(zi * za, 8), za)
    blk_b = pl.ds(pl.multiple_of(half + yi * ya, 8), ya)
    g1, g2 = {}, {}
    for slot in order:
        for c in xs[slot]:
            c.wait()
        g1[slot] = []
        for k, peers, n, rows in ((0, [(d, dev(y=y)) for d, y in ypeer], ny, own_a), (1, [(d, dev(z=z)) for d, z in zpeer], nz, own_b)):
            for d, who in peers:
                ref = pf.at[slot, rows, pcols]
                g1[slot].append(remote(ref, ref, g_send.at[k, slot - 1, d - 1], g_recv.at[k, slot - 1, n - d - 1], who))
        for c in g1[slot]:
            c.start()
    norm_and_send(cuts[1], cuts[2])
    for slot in order:
        for c in g1[slot]:
            c.wait()
        g2[slot] = []
        for k, peers, n, rows in ((2, [(d, dev(z=z)) for d, z in zpeer], nz, blk_a), (3, [(d, dev(y=y)) for d, y in ypeer], ny, blk_b)):
            for d, who in peers:
                ref = pf.at[slot, rows, pcols]
                g2[slot].append(remote(ref, ref, g_send.at[k, slot - 1, d - 1], g_recv.at[k, slot - 1, n - d - 1], who))
        for c in g2[slot]:
            c.start()
    norm_and_send(cuts[2], npl)
    w_copy.wait()

    col = (tp * cols + lane_ids((1, cols))).astype(F32)
    valid = col < float(VALID_CLASSES)
    vweight = jnp.where(valid, SMOOTH / VALID_CLASSES, 0.0)
    sub = 32

    def col_of(packed, lane):
        return jnp.sum(jnp.where(lane8 == lane, packed, 0.0), axis=-1, keepdims=True)

    def label_col(slot, r):
        return jnp.concatenate([col_of(labs[slot], r * (sub // 8) + k) for k in range(sub // 8)], axis=0)

    stat[tp] = jnp.zeros_like(stat[0])
    bias = b_ref[...].reshape(1, cols)

    def logits_of(slot):
        xabs = lax.rem(xi + slot, nx)
        p16[xabs] = pf[slot].astype(BF16)
        lg[xabs] = jnp.dot(p16[xabs], w[...], preferred_element_type=F32)

        def body(r, _):
            rows = pl.ds(pl.multiple_of(r * sub, sub), sub)
            l = jnp.where(valid, lg[xabs, rows, :] + bias, -1e30)
            m = jnp.max(l, axis=-1, keepdims=True)
            e = jnp.exp(l - m)
            s = jnp.sum(e, axis=-1, keepdims=True)
            lg[xabs, rows, :] = e
            hot = col == label_col(slot, r)
            part = jnp.where(hot, (1.0 - SMOOTH) * l, 0.0) + vweight * l
            ps = jnp.sum(part, axis=-1, keepdims=True)
            ms, ss, pp = stat[tp, 0], stat[tp, 1], stat[tp, 2]
            for k in range(sub // 8):
                here = lane8 == xabs * groups + r * (sub // 8) + k
                ms = jnp.where(here, m[8 * k : 8 * k + 8], ms)
                ss = jnp.where(here, s[8 * k : 8 * k + 8], ss)
                pp = jnp.where(here, ps[8 * k : 8 * k + 8], pp)
            stat[tp, 0], stat[tp, 1], stat[tp, 2] = ms, ss, pp
            return 0

        lax.fori_loop(0, ti // sub, body, 0)

    logits_of(0)
    for slot in order:
        for c in g2[slot]:
            c.wait()
        ref = pf.at[slot, :, dcols]
        whole = remote(ref, ref, xd_send.at[nx - slot - 1], xd_recv.at[slot - 1], dev(x=xpeer[slot - 1][1]))
        whole.wait_recv()
        logits_of(slot)
    mine_m = stat[tp, 0]

    st1 = [remote(stat.at[tp], stat.at[tp], s_send.at[k - 1], s_recv.at[k - 1], who) for k, who in plane]
    for c in st1:
        c.start()
    for slot in order:
        ref = pf.at[slot, :, dcols]
        remote(ref, ref, xd_send.at[slot - 1], xd_recv.at[slot - 1], dev(x=xpeer[slot - 1][1])).wait_send()
    for c in st1:
        c.wait()
    m = stat[0, 0]
    for k in range(1, npl):
        m = jnp.maximum(m, stat[k, 0])
    s = jnp.zeros_like(m)
    q = jnp.zeros_like(m)
    for k in range(npl):
        s = s + stat[k, 1] * jnp.exp(stat[k, 0] - m)
        q = q + stat[k, 2]
    used = lane8 < nx * groups
    coef = jnp.where(used, jnp.exp(mine_m - m) / s * (1.0 / rows_total), 0.0)
    loss_rows = jnp.where(used, m + jnp.log(jnp.where(used, s, 1.0)) - q, 0.0)
    cof[...] = coef
    vscaled = vweight * (1.0 / rows_total)
    hotscaled = (1.0 - SMOOTH) / rows_total

    def dlogit_of(slot, acc):
        xabs = lax.rem(xi + slot, nx)

        def body(r, acc):
            rows = pl.ds(pl.multiple_of(r * sub, sub), sub)
            cc = cof[...]
            cf = jnp.concatenate([col_of(cc, xabs * groups + r * (sub // 8) + k) for k in range(sub // 8)], axis=0)
            hot = col == label_col(slot, r)
            dl = lg[xabs, rows, :] * cf - jnp.where(hot, hotscaled, 0.0) - vscaled
            dl16[xabs, rows, :] = dl.astype(BF16)
            lg[xabs, rows, :] = dl
            return acc

        return lax.fori_loop(0, ti // sub, body, acc)

    dlogit_of(0, 0)
    dpp[...] = lax.dot_general(dl16[xi], w[...], (((1,), (1,)), ((), ())), preferred_element_type=F32)

    r1 = []
    for d, z in zpeer:
        r1.append(remote(dpp.at[pl.ds(pl.multiple_of(z * za, 8), za)], ra.at[nz - d - 1], r_send.at[0, d - 1], r_recv.at[0, nz - d - 1], dev(z=z)))
    for d, y in ypeer:
        r1.append(remote(dpp.at[pl.ds(pl.multiple_of(half + y * ya, 8), ya)], rb.at[ny - d - 1], r_send.at[1, d - 1], r_recv.at[1, ny - d - 1], dev(y=y)))
    for c in r1:
        c.start()
    lax.fori_loop(1, nx, lambda s, a: dlogit_of(s, a), 0)

    for c in r1:
        c.wait()

    def total(buf, own, n):
        t = own
        for k in range(n - 1):
            t = t + buf[k]
        return t

    ta[...] = total(ra, dpp[blk_a, :], nz)
    tb[...] = total(rb, dpp[blk_b, :], ny)
    r2 = []
    for d, y in ypeer:
        r2.append(remote(ta.at[pl.ds(pl.multiple_of(y * pb, 8), pb)], ra2.at[ny - d - 1], r_send.at[2, d - 1], r_recv.at[2, ny - d - 1], dev(y=y)))
    for d, z in zpeer:
        r2.append(remote(tb.at[pl.ds(pl.multiple_of(z * pb, 8), pb)], rb2.at[nz - d - 1], r_send.at[3, d - 1], r_recv.at[3, nz - d - 1], dev(z=z)))
    for c in r2:
        c.start()

    mh = width // 2

    def dw_half(h, out):
        lhs_cols = pl.ds(pl.multiple_of(h * mh, 128), mh)
        k = nx * ti
        out[...] = lax.dot_general(p16[:, :, lhs_cols].reshape(k, mh), dl16[...].reshape(k, cols), (((0,), (0,)), ((), ())), preferred_element_type=F32)

    dw_half(1 - ci, dwpart)
    ex = remote(dwpart, dwrecv, d_send.at[0], d_recv.at[0], dev(c=1 - ci))
    ex.start()
    for c in r2:
        c.wait()
    dpf[own_a, :] = total(ra2, ta[pl.ds(pl.multiple_of(yi * pb, 8), pb), :], ny)
    dpf[own_b, :] = total(rb2, tb[pl.ds(pl.multiple_of(zi * pb, 8), pb), :], nz)
    gy[yi, 0:1, :] = jnp.sum(dpf[own_a, :] * xm[own_a, :] + dpf[own_b, :] * xm[own_b, :], axis=0, keepdims=True)
    gy[yi, 1:2, :] = jnp.sum(dpf[own_a, :] + dpf[own_b, :], axis=0, keepdims=True)
    a1 = []
    for d, y in ypeer:
        a1.append(remote(dpf.at[own_a], dpf.at[own_a], r_send.at[4, d - 1], r_recv.at[4, ny - d - 1], dev(y=y)))
    for d, z in zpeer:
        a1.append(remote(dpf.at[own_b], dpf.at[own_b], r_send.at[5, d - 1], r_recv.at[5, nz - d - 1], dev(z=z)))
    for d, y in ypeer:
        a1.append(remote(gy.at[yi], gy.at[yi], q_send.at[0, d - 1], q_recv.at[0, ny - d - 1], dev(y=y)))
    for c in a1:
        c.start()
    dw_half(ci, dwbuf.at[0])

    def dbody(r, acc):
        return acc + lg[r // groups, pl.ds(pl.multiple_of(lax.rem(r, groups) * 8, 8), 8), :]

    db8 = lax.fori_loop(0, nx * groups, dbody, jnp.zeros((8, cols), F32))
    for c in a1:
        c.wait()
    a2 = []
    for d, z in zpeer:
        a2.append(remote(dpf.at[blk_a], dpf.at[blk_a], r_send.at[6, d - 1], r_recv.at[6, nz - d - 1], dev(z=z)))
    for d, y in ypeer:
        a2.append(remote(dpf.at[blk_b], dpf.at[blk_b], r_send.at[7, d - 1], r_recv.at[7, ny - d - 1], dev(y=y)))

    def summed(buf, n):
        t = buf[0]
        for k in range(1, n):
            t = t + buf[k]
        return t

    gz[zi] = summed(gy, ny)
    t1 = [remote(gz.at[zi], gz.at[zi], q_send.at[1, d - 1], q_recv.at[1, nz - d - 1], dev(z=z)) for d, z in zpeer]
    for c in t1 + a2:
        c.start()
    ex.wait()
    dwbuf[0] = dwbuf[0] + dwrecv[...]
    back = remote(dwbuf.at[0], dwbuf.at[1], d_send.at[1], d_recv.at[1], dev(c=1 - ci))
    back.start()
    for c in t1:
        c.wait()
    gx[xi] = summed(gz, nz)
    t2 = [remote(gx.at[xi], gx.at[xi], q_send.at[2, d - 1], q_recv.at[2, nx - d - 1], dev(x=x)) for d, x in xpeer]
    for c in t2:
        c.start()
    gc[0] = jnp.zeros_like(gc[0])
    gc[0, 0:1, width : width + cols] = jnp.sum(db8, axis=0, keepdims=True)
    gc[0, :, width + cols :] = loss_rows
    for c in t2:
        c.wait()
    gc[0, :, 0:width] = summed(gx, nx)
    t3 = remote(gc.at[0], gc.at[1], q_send.at[3, 0], q_recv.at[3, 0], dev(c=1 - ci))
    t3.start()
    for c in a2:
        c.wait()
    t3.wait()
    small_ref[...] = gc[0] + gc[1]
    back.wait()


def norm_bwd_kernel(rows_total, f_ref, dp_ref, gam_ref, st_ref, dwin_ref, small_ref, out_ref, dw_ref, loss_ref, db_ref, dg_ref, dbt_ref):
    tokens, rows, width = f_ref.shape
    cols = db_ref.shape[0]
    i = pl.program_id(0)
    ids = lane_ids((tokens, 8, LANES))

    def one(h, _):
        r = pl.ds(pl.multiple_of(h * 8, 8), 8)
        blk = i * (rows // 8) + h
        u = dp_ref[r, :] * gam_ref[...] * (1.0 / tokens)
        ut = u - jnp.mean(u, axis=-1, keepdims=True)
        st = st_ref[...]
        mean = jnp.sum(jnp.where(ids == blk, st, 0.0), axis=-1, keepdims=True)
        inv = jnp.sum(jnp.where(ids == blk + 64, st, 0.0), axis=-1, keepdims=True)
        cen = f_ref[:, r, :].astype(F32) - mean
        proj = jnp.sum(cen * ut[None], axis=-1, keepdims=True) * inv * (1.0 / width)
        out_ref[:, r, :] = (inv * (ut[None] - cen * (inv * proj))).astype(BF16)
        return 0

    lax.fori_loop(0, rows // 8, one, 0)
    dr = dw_ref.shape[0]
    per = width // 2 // dr
    own = (i // per) == lax.rem(lax.axis_index("dp"), 2)
    dw_ref[...] = dwin_ref[jnp.where(own, 0, 1), pl.ds(pl.multiple_of(lax.rem(i, per) * dr, 8), dr), :]

    @pl.when(i == 0)
    def _():
        dg_ref[...] = small_ref[0:1, 0:width].reshape(width)
        dbt_ref[...] = small_ref[1:2, 0:width].reshape(width)
        db_ref[...] = small_ref[0:1, width : width + cols].reshape(cols)
        tail = jnp.sum(jnp.sum(small_ref[:, width + cols :], axis=-1, keepdims=True), axis=0, keepdims=True)
        loss_ref[...] = tail * (1.0 / rows_total)


def solution(mesh):
    sides = SIDES[mesh.devices.size]
    nx, ny, nz = sides
    dp_size = mesh.shape["dp"]

    def local_head(feats, ln_gamma, ln_beta, w_head, b_head, labels):
        ti, tokens, width = feats.shape
        cols = w_head.shape[1]
        half = ti // 2
        pb = half // (ny * nz)
        ft = jnp.transpose(feats, (1, 0, 2))
        gam, bet = ln_gamma[None], ln_beta[None]
        vm = pl.BlockSpec(memory_space=pltpu.VMEM)
        hbm = pl.BlockSpec(memory_space=pl.ANY)
        sm = pl.BlockSpec(memory_space=pltpu.SMEM)
        sem = pltpu.SemaphoreType.DMA
        n3 = max(nx, ny, nz)
        npl = ny * nz
        S = jax.ShapeDtypeStruct
        extra = width + cols + LANES
        dw, small, dpool, st = pl.pallas_call(
            functools.partial(head_kernel, sides, ti * dp_size),
            out_shape=(pltpu.VMEM((2, width // 2, cols), F32), pltpu.VMEM((8, extra), F32), pltpu.VMEM((ti, width), F32), pltpu.VMEM((tokens, 8, LANES), F32)),
            in_specs=[hbm, vm, vm, hbm, vm, sm],
            out_specs=(vm, vm, vm, vm),
            scratch_shapes=[
                pltpu.VMEM((min(4, npl), 2, tokens, pb, width), BF16),
                pltpu.VMEM((width, cols), BF16),
                pltpu.VMEM((nx, ti, width), F32),
                pltpu.VMEM((nx, ti, width), BF16),
                pltpu.VMEM((nx, ti, cols), F32),
                pltpu.VMEM((nx, ti, cols), BF16),
                pltpu.VMEM((width // 2, cols), F32),
                pltpu.VMEM((width // 2, cols), F32),
                pltpu.VMEM((ti, width), F32),
                pltpu.VMEM((ti, width), F32),
                pltpu.VMEM((nx, 8, LANES), F32),
                pltpu.VMEM((nz - 1, half // nz, width), F32),
                pltpu.VMEM((ny - 1, half // ny, width), F32),
                pltpu.VMEM((ny - 1, pb, width), F32),
                pltpu.VMEM((nz - 1, pb, width), F32),
                pltpu.VMEM((half // nz, width), F32),
                pltpu.VMEM((half // ny, width), F32),
                pltpu.VMEM((npl, 3, 8, LANES), F32),
                pltpu.VMEM((8, LANES), F32),
                pltpu.VMEM((ny, 8, width), F32),
                pltpu.VMEM((nz, 8, width), F32),
                pltpu.VMEM((nx, 8, width), F32),
                pltpu.VMEM((2, 8, extra), F32),
                sem((min(4, npl), 2)),
                sem,
                sem((nx - 1, 2)), sem((nx - 1, 2)), sem((nx - 1,)), sem((nx - 1,)), sem((nx - 1,)), sem((nx - 1,)),
                sem((4, nx - 1, n3 - 1)), sem((4, nx - 1, n3 - 1)),
                sem((npl - 1,)), sem((npl - 1,)),
                sem((8, n3 - 1)), sem((8, n3 - 1)),
                sem((2,)), sem((2,)),
                sem((4, n3 - 1)), sem((4, n3 - 1)),
            ],
            compiler_params=pltpu.CompilerParams(collective_id=0, has_side_effects=True, vmem_limit_bytes=48 * 1024 * 1024),
        )(ft, gam, bet, w_head, b_head, labels)
        rb = 16
        steps = ti // rb
        near = lambda a: pltpu.with_memory_space_constraint(a, pltpu.VMEM)
        dft, dwo, loss, db, dg, dbt = pl.pallas_call(
            functools.partial(norm_bwd_kernel, ti * dp_size),
            grid=(steps,),
            out_shape=(S((tokens, ti, width), BF16), S((width, cols), F32), S((1, 1), F32), S((cols,), F32), S((width,), F32), S((width,), F32)),
            in_specs=[
                pl.BlockSpec((tokens, rb, width), lambda i: (0, i, 0)),
                pl.BlockSpec((rb, width), lambda i: (i, 0)),
                pl.BlockSpec((1, width), lambda i: (0, 0)),
                vm, vm, vm,
            ],
            out_specs=(
                pl.BlockSpec((tokens, rb, width), lambda i: (0, i, 0)),
                pl.BlockSpec((width // steps, cols), lambda i: (i, 0)),
                vm, vm, vm, vm,
            ),
            compiler_params=pltpu.CompilerParams(vmem_limit_bytes=40 * 1024 * 1024),
        )(ft, dpool, gam, near(st), near(dw), near(small))
        return loss[0, 0], jnp.transpose(dft, (1, 0, 2)), dwo, db, dg, dbt

    return jax.shard_map(
        local_head,
        mesh=mesh,
        in_specs=(P("dp", None, None), P(), P(), P(None, "tp"), P("tp"), P("dp")),
        out_specs=(P(), P("dp", None, None), P(None, "tp"), P("tp"), P(), P()),
        check_vma=False,
    )
```

time: 123 us -> 101 us (0.82)
  Pallas kernels: 111 us -> 99.8 us
  local copies, waits for them, and re-layouts: 9.12 us -> 0.01 us
  other arithmetic: 1.99 us -> 0 us
    pallas_call x1, Pallas kernels: 88.1 us -> 75.9 us  [local_head(): pl.pallas_call(functools.partial(head_kernel, sides, ti * dp_size), out_s...]
    unnamed x15 -> x2, local copies, waits for them, and re-layouts: 5.87 us -> 0.01 us
    pallas_call x1 -> x0, other arithmetic: 1.31 us -> none  [local_head(): pl.pallas_call(functools.partial(head_kernel, sides, ti * dp_size), out_s...]
    broadcast_in_dim x1 -> x0, local copies, waits for them, and re-layouts: 1.29 us -> none  [local_head(): gam, bet, bias = (ln_gamma[None], ln_beta[None], b_head[None])]
    pallas_call x1, Pallas kernels: 22.6 us -> 23.9 us  [local_head(): pl.pallas_call(functools.partial(norm_bwd_kernel, ti * dp_size), grid=(st...]
where the time goes in v2:
time: 101 us; the launch traced here: 100 us
  Pallas kernels  99.8 us (99%)
    pallas_call x1, Pallas kernels, local_head(): pl.pallas_call(functools.partial(head_kernel, sides, ti * dp_size), out_s...  75.9 us
    pallas_call x1, Pallas kernels, local_head(): pl.pallas_call(functools.partial(norm_bwd_kernel, ti * dp_size), grid=(st...  23.9 us

profile of v2, /device:TPU:1, one launch (start us, length us, event | category | flops | bytes accessed | tf_op | source)
XLA Modules:
  0.0 100.4 jit_solution(12177427146386986766)
XLA Ops:
  0.6 0.0 copy-start
  0.6 75.9 %shard_map.109 = (f32[2,512,1408]{2,1,0:T(8,128)S(1)}, f32[8,2560]{1,0:T(8,128)S(1)}, f32[256,1024]{1,0:T(8,128)S(1)}, f32[36,8,128]{2,1,0:T(8,128)S(1)}) custom-call(bf16[36,256,1024]{2,1,0:T(8,128)(2,1)} %bitcast.7, f32[1,1024]{1,0:T(1,128)} %bitcast.5, f32[1,1024]{1,0:T(1,128)} %bitcast.9, bf16[1024,1408]{1,0:T(8,128)(2,1)} %w_hbm.1, f32[1408]{0:T(1024)} %b_ref.1, ...), custom_call_target="tpu_custom_call" | custom-call | tf_op jit(solution)/shard_map/pallas_call | solution.py:435
  76.5 0.0 copy-done
  76.6 23.9 %shard_map.110 = (bf16[36,256,1024]{2,1,0:T(8,128)(2,1)}, f32[1024,1408]{1,0:T(8,128)}, f32[1,1]{1,0:T(1,128)}, f32[1408]{0:T(1024)}, f32[1024]{0:T(1024)}, /*index=5*/f32[1024]{0:T(1024)}) custom-call(bf16[36,256,1024]{2,1,0:T(8,128)(2,1)} %bitcast.8, f32[256,1024]{1,0:T(8,128)S(1)} %get-tuple-element.16.dp_ref, f32[1,1024]{1,0:T(1,128)S(1)} %bitcast.6, ...), custom_call_target="tpu_custom_call" | custom-call | tf_op jit(solution)/shard_map/pallas_call | solution.py:478
Async XLA Ops:
  0.6 75.9 %copy-start = (f32[1024]{0:T(1024)S(1)}, f32[1024]{0:T(1024)}, u32[]{:S(2)}) copy-start(f32[1024]{0:T(1024)} %param.7) | copy-start | bytes 12292

commit v3 on v2

--- a/solution.py
+++ b/solution.py
@@ -24,9 +24,9 @@
 def head_kernel(
     sides, rows_total, f_ref, gam_ref, bet_ref, w_hbm, b_ref, lab_ref,
     dwbuf, small_ref, dpf, st_ref,
-    fbuf, w, pf, p16, lg, dl16, dwpart, dwrecv, xm, dpp, labs,
-    ra, rb, ra2, rb2, ta, tb, stat, cof, gy, gz, gx, gc,
-    f_sem, w_sem, x_send, x_recv, xl_send, xl_recv, xd_send, xd_recv, g_send, g_recv, s_send, s_recv,
+    fbuf, w, pf, p16, lt, lg, dl16, dwpart, dwrecv, xm, dpp, labs,
+    ra, rb, ra2, rb2, ta, tb, near, stat, cof, dbs, gy, gz, gx, gc,
+    f_sem, w_sem, x_send, x_recv, xl_send, xl_recv, xd_send, xd_recv, g_send, g_recv, n_send, n_recv, s_send, s_recv,
     r_send, r_recv, d_send, d_recv, q_send, q_recv,
 ):
     nx, ny, nz = sides
@@ -188,92 +188,87 @@
     col = (tp * cols + lane_ids((1, cols))).astype(F32)
     valid = col < float(VALID_CLASSES)
     vweight = jnp.where(valid, SMOOTH / VALID_CLASSES, 0.0)
-    sub = 32
+    sub = min(64, ti)
 
     def col_of(packed, lane):
         return jnp.sum(jnp.where(lane8 == lane, packed, 0.0), axis=-1, keepdims=True)
 
-    def label_col(slot, r):
-        return jnp.concatenate([col_of(labs[slot], r * (sub // 8) + k) for k in range(sub // 8)], axis=0)
-
+    def cols_of(packed, lane):
+        return jnp.concatenate([col_of(packed, lane + k) for k in range(sub // 8)], axis=0)
+
+    near[tp] = jnp.zeros_like(near[0])
     stat[tp] = jnp.zeros_like(stat[0])
     bias = b_ref[...].reshape(1, cols)
 
-    def logits_of(slot):
+    def logits_of(slot, out):
         xabs = lax.rem(xi + slot, nx)
         p16[xabs] = pf[slot].astype(BF16)
-        lg[xabs] = jnp.dot(p16[xabs], w[...], preferred_element_type=F32)
-
-        def body(r, _):
+        lt[...] = jnp.dot(p16[xabs], w[...], preferred_element_type=F32)
+
+        def body(r, carry):
+            ms, ss, pp = carry
             rows = pl.ds(pl.multiple_of(r * sub, sub), sub)
-            l = jnp.where(valid, lg[xabs, rows, :] + bias, -1e30)
+            l = jnp.where(valid, lt[rows, :] + bias, -1e30)
             m = jnp.max(l, axis=-1, keepdims=True)
             e = jnp.exp(l - m)
             s = jnp.sum(e, axis=-1, keepdims=True)
             lg[xabs, rows, :] = e
-            hot = col == label_col(slot, r)
-            part = jnp.where(hot, (1.0 - SMOOTH) * l, 0.0) + vweight * l
-            ps = jnp.sum(part, axis=-1, keepdims=True)
-            ms, ss, pp = stat[tp, 0], stat[tp, 1], stat[tp, 2]
+            hot = col == cols_of(labs[slot], r * (sub // 8))
+            ps = jnp.sum(jnp.where(hot, vweight + (1.0 - SMOOTH), vweight) * l, axis=-1, keepdims=True)
             for k in range(sub // 8):
                 here = lane8 == xabs * groups + r * (sub // 8) + k
                 ms = jnp.where(here, m[8 * k : 8 * k + 8], ms)
                 ss = jnp.where(here, s[8 * k : 8 * k + 8], ss)
                 pp = jnp.where(here, ps[8 * k : 8 * k + 8], pp)
-            stat[tp, 0], stat[tp, 1], stat[tp, 2] = ms, ss, pp
-            return 0
-
-        lax.fori_loop(0, ti // sub, body, 0)
-
-    logits_of(0)
-    for slot in order:
+            return ms, ss, pp
+
+        ms, ss, pp = lax.fori_loop(0, ti // sub, body, (out[tp, 0], out[tp, 1], stat[tp, 2]))
+        out[tp, 0], out[tp, 1], stat[tp, 2] = ms, ss, pp
+
+    def gathered(slot):
         for c in g2[slot]:
             c.wait()
         ref = pf.at[slot, :, dcols]
-        whole = remote(ref, ref, xd_send.at[nx - slot - 1], xd_recv.at[slot - 1], dev(x=xpeer[slot - 1][1]))
-        whole.wait_recv()
-        logits_of(slot)
-    mine_m = stat[tp, 0]
-
-    st1 = [remote(stat.at[tp], stat.at[tp], s_send.at[k - 1], s_recv.at[k - 1], who) for k, who in plane]
-    for c in st1:
-        c.start()
-    for slot in order:
-        ref = pf.at[slot, :, dcols]
-        remote(ref, ref, xd_send.at[slot - 1], xd_recv.at[slot - 1], dev(x=xpeer[slot - 1][1])).wait_send()
-    for c in st1:
-        c.wait()
-    m = stat[0, 0]
-    for k in range(1, npl):
-        m = jnp.maximum(m, stat[k, 0])
-    s = jnp.zeros_like(m)
-    q = jnp.zeros_like(m)
-    for k in range(npl):
-        s = s + stat[k, 1] * jnp.exp(stat[k, 0] - m)
-        q = q + stat[k, 2]
-    used = lane8 < nx * groups
-    coef = jnp.where(used, jnp.exp(mine_m - m) / s * (1.0 / rows_total), 0.0)
-    loss_rows = jnp.where(used, m + jnp.log(jnp.where(used, s, 1.0)) - q, 0.0)
-    cof[...] = coef
+        remote(ref, ref, xd_send.at[nx - slot - 1], xd_recv.at[slot - 1], dev(x=xpeer[slot - 1][1])).wait_recv()
+        logits_of(slot, stat)
+
+    def merged(buf, used):
+        m = buf[0, 0]
+        for k in range(1, npl):
+            m = jnp.maximum(m, buf[k, 0])
+        s = jnp.zeros_like(m)
+        for k in range(npl):
+            s = s + buf[k, 1] * jnp.exp(buf[k, 0] - m)
+        coef = jnp.where(used, jnp.exp(buf[tp, 0] - m) / s * (1.0 / rows_total), 0.0)
+        return coef, jnp.where(used, m + jnp.log(jnp.where(used, s, 1.0)), 0.0)
+
     vscaled = vweight * (1.0 / rows_total)
-    hotscaled = (1.0 - SMOOTH) / rows_total
-
-    def dlogit_of(slot, acc):
+    vhot = vscaled + (1.0 - SMOOTH) / rows_total
+
+    def dlogit_of(slot):
         xabs = lax.rem(xi + slot, nx)
 
         def body(r, acc):
             rows = pl.ds(pl.multiple_of(r * sub, sub), sub)
-            cc = cof[...]
-            cf = jnp.concatenate([col_of(cc, xabs * groups + r * (sub // 8) + k) for k in range(sub // 8)], axis=0)
-            hot = col == label_col(slot, r)
-            dl = lg[xabs, rows, :] * cf - jnp.where(hot, hotscaled, 0.0) - vscaled
+            cf = cols_of(cof[...], xabs * groups + r * (sub // 8))
+            hot = col == cols_of(labs[slot], r * (sub // 8))
+            dl = lg[xabs, rows, :] * cf - jnp.where(hot, vhot, vscaled)
             dl16[xabs, rows, :] = dl.astype(BF16)
-            lg[xabs, rows, :] = dl
-            return acc
-
-        return lax.fori_loop(0, ti // sub, body, acc)
-
-    dlogit_of(0, 0)
+            return acc + jnp.sum(dl.reshape(sub // 8, 8, cols), axis=0)
+
+        dbs[xabs] = lax.fori_loop(0, ti // sub, body, jnp.zeros((8, cols), F32))
+
+    lane_block = lane8 // groups
+    logits_of(0, near)
+    st0 = [remote(near.at[tp], near.at[tp], n_send.at[k - 1], n_recv.at[k - 1], who) for k, who in plane]
+    for c in st0:
+        c.start()
+    gathered(order[0])
+    for c in st0:
+        c.wait()
+    coef, lse0 = merged(near, lane_block == xi)
+    cof[...] = coef
+    dlogit_of(0)
     dpp[...] = lax.dot_general(dl16[xi], w[...], (((1,), (1,)), ((), ())), preferred_element_type=F32)
 
     r1 = []
@@ -283,7 +278,14 @@
         r1.append(remote(dpp.at[pl.ds(pl.multiple_of(half + y * ya, 8), ya)], rb.at[ny - d - 1], r_send.at[1, d - 1], r_recv.at[1, ny - d - 1], dev(y=y)))
     for c in r1:
         c.start()
-    lax.fori_loop(1, nx, lambda s, a: dlogit_of(s, a), 0)
+    for slot in order[1:]:
+        gathered(slot)
+    st1 = [remote(stat.at[tp], stat.at[tp], s_send.at[k - 1], s_recv.at[k - 1], who) for k, who in plane]
+    for c in st1:
+        c.start()
+    for slot in order:
+        ref = pf.at[slot, :, dcols]
+        remote(ref, ref, xd_send.at[slot - 1], xd_recv.at[slot - 1], dev(x=xpeer[slot - 1][1])).wait_send()
 
     for c in r1:
         c.wait()
@@ -311,9 +313,6 @@
         k = nx * ti
         out[...] = lax.dot_general(p16[:, :, lhs_cols].reshape(k, mh), dl16[...].reshape(k, cols), (((0,), (0,)), ((), ())), preferred_element_type=F32)
 
-    dw_half(1 - ci, dwpart)
-    ex = remote(dwpart, dwrecv, d_send.at[0], d_recv.at[0], dev(c=1 - ci))
-    ex.start()
     for c in r2:
         c.wait()
     dpf[own_a, :] = total(ra2, ta[pl.ds(pl.multiple_of(yi * pb, 8), pb), :], ny)
@@ -329,12 +328,14 @@
         a1.append(remote(gy.at[yi], gy.at[yi], q_send.at[0, d - 1], q_recv.at[0, ny - d - 1], dev(y=y)))
     for c in a1:
         c.start()
-    dw_half(ci, dwbuf.at[0])
-
-    def dbody(r, acc):
-        return acc + lg[r // groups, pl.ds(pl.multiple_of(lax.rem(r, groups) * 8, 8), 8), :]
-
-    db8 = lax.fori_loop(0, nx * groups, dbody, jnp.zeros((8, cols), F32))
+    for c in st1:
+        c.wait()
+    coef, lse1 = merged(stat, (lane_block != xi) & (lane_block < nx))
+    loss_rows = lse0 + lse1
+    for k in range(npl):
+        loss_rows = loss_rows - stat[k, 2]
+    cof[...] = coef
+    dlogit_of(order[0])
     for c in a1:
         c.wait()
     a2 = []
@@ -353,18 +354,24 @@
     t1 = [remote(gz.at[zi], gz.at[zi], q_send.at[1, d - 1], q_recv.at[1, nz - d - 1], dev(z=z)) for d, z in zpeer]
     for c in t1 + a2:
         c.start()
+    for slot in order[1:]:
+        dlogit_of(slot)
+    dw_half(1 - ci, dwpart)
+    ex = remote(dwpart, dwrecv, d_send.at[0], d_recv.at[0], dev(c=1 - ci))
+    ex.start()
+    dw_half(ci, dwbuf.at[0])
+    for c in t1:
+        c.wait()
+    gx[xi] = summed(gz, nz)
+    t2 = [remote(gx.at[xi], gx.at[xi], q_send.at[2, d - 1], q_recv.at[2, nx - d - 1], dev(x=x)) for d, x in xpeer]
+    for c in t2:
+        c.start()
     ex.wait()
     dwbuf[0] = dwbuf[0] + dwrecv[...]
     back = remote(dwbuf.at[0], dwbuf.at[1], d_send.at[1], d_recv.at[1], dev(c=1 - ci))
     back.start()
-    for c in t1:
-        c.wait()
-    gx[xi] = summed(gz, nz)
-    t2 = [remote(gx.at[xi], gx.at[xi], q_send.at[2, d - 1], q_recv.at[2, nx - d - 1], dev(x=x)) for d, x in xpeer]
-    for c in t2:
-        c.start()
     gc[0] = jnp.zeros_like(gc[0])
-    gc[0, 0:1, width : width + cols] = jnp.sum(db8, axis=0, keepdims=True)
+    gc[0, 0:1, width : width + cols] = jnp.sum(summed(dbs, nx), axis=0, keepdims=True)
     gc[0, :, width + cols :] = loss_rows
     for c in t2:
         c.wait()
@@ -442,6 +449,7 @@
                 pltpu.VMEM((width, cols), BF16),
                 pltpu.VMEM((nx, ti, width), F32),
                 pltpu.VMEM((nx, ti, width), BF16),
+                pltpu.VMEM((ti, cols), F32),
                 pltpu.VMEM((nx, ti, cols), F32),
                 pltpu.VMEM((nx, ti, cols), BF16),
                 pltpu.VMEM((width // 2, cols), F32),
@@ -455,8 +463,10 @@
                 pltpu.VMEM((nz - 1, pb, width), F32),
                 pltpu.VMEM((half // nz, width), F32),
                 pltpu.VMEM((half // ny, width), F32),
+                pltpu.VMEM((npl, 2, 8, LANES), F32),
                 pltpu.VMEM((npl, 3, 8, LANES), F32),
                 pltpu.VMEM((8, LANES), F32),
+                pltpu.VMEM((nx, 8, cols), F32),
                 pltpu.VMEM((ny, 8, width), F32),
                 pltpu.VMEM((nz, 8, width), F32),
                 pltpu.VMEM((nx, 8, width), F32),
@@ -465,12 +475,12 @@
                 sem,
                 sem((nx - 1, 2)), sem((nx - 1, 2)), sem((nx - 1,)), sem((nx - 1,)), sem((nx - 1,)), sem((nx - 1,)),
                 sem((4, nx - 1, n3 - 1)), sem((4, nx - 1, n3 - 1)),
-                sem((npl - 1,)), sem((npl - 1,)),
+                sem((npl - 1,)), sem((npl - 1,)), sem((npl - 1,)), sem((npl - 1,)),
                 sem((8, n3 - 1)), sem((8, n3 - 1)),
                 sem((2,)), sem((2,)),
                 sem((4, n3 - 1)), sem((4, n3 - 1)),
             ],
-            compiler_params=pltpu.CompilerParams(collective_id=0, has_side_effects=True, vmem_limit_bytes=48 * 1024 * 1024),
+            compiler_params=pltpu.CompilerParams(collective_id=0, has_side_effects=True, vmem_limit_bytes=50 * 1024 * 1024),
         )(ft, gam, bet, w_head, b_head, labels)
         rb = 16
         steps = ti // rb

time: 101 us -> 97.5 us (0.965)
  Pallas kernels: 99.8 us -> 96.2 us
    pallas_call x1, Pallas kernels: 75.9 us -> 72.3 us  [local_head(): pl.pallas_call(functools.partial(head_kernel, sides, ti * dp_size), out_s...]
where the time goes in v3:
time: 97.5 us; the launch traced here: 96.9 us
  Pallas kernels  96.2 us (99%)
    pallas_call x1, Pallas kernels, local_head(): pl.pallas_call(functools.partial(head_kernel, sides, ti * dp_size), out_s...  72.3 us
    pallas_call x1, Pallas kernels, local_head(): pl.pallas_call(functools.partial(norm_bwd_kernel, ti * dp_size), grid=(st...  23.9 us

profile of v3, /device:TPU:1, one launch (start us, length us, event | category | flops | bytes accessed | tf_op | source)
XLA Modules:
  0.0 96.9 jit_solution(18310160074627764352)
XLA Ops:
  0.6 0.0 copy-start
  0.6 72.3 %shard_map.109 = (f32[2,512,1408]{2,1,0:T(8,128)S(1)}, f32[8,2560]{1,0:T(8,128)S(1)}, f32[256,1024]{1,0:T(8,128)S(1)}, f32[36,8,128]{2,1,0:T(8,128)S(1)}) custom-call(bf16[36,256,1024]{2,1,0:T(8,128)(2,1)} %bitcast.7, f32[1,1024]{1,0:T(1,128)} %bitcast.5, f32[1,1024]{1,0:T(1,128)} %bitcast.9, bf16[1024,1408]{1,0:T(8,128)(2,1)} %w_hbm.1, f32[1408]{0:T(1024)} %b_ref.1, ...), custom_call_target="tpu_custom_call" | custom-call | tf_op jit(solution)/shard_map/pallas_call | solution.py:442
  73.0 0.0 copy-done
  73.0 23.9 %shard_map.110 = (bf16[36,256,1024]{2,1,0:T(8,128)(2,1)}, f32[1024,1408]{1,0:T(8,128)}, f32[1,1]{1,0:T(1,128)}, f32[1408]{0:T(1024)}, f32[1024]{0:T(1024)}, /*index=5*/f32[1024]{0:T(1024)}) custom-call(bf16[36,256,1024]{2,1,0:T(8,128)(2,1)} %bitcast.8, f32[256,1024]{1,0:T(8,128)S(1)} %get-tuple-element.16.dp_ref, f32[1,1024]{1,0:T(1,128)S(1)} %bitcast.6, ...), custom_call_target="tpu_custom_call" | custom-call | tf_op jit(solution)/shard_map/pallas_call | solution.py:488
Async XLA Ops:
  0.6 72.3 %copy-start = (f32[1024]{0:T(1024)S(1)}, f32[1024]{0:T(1024)}, u32[]{:S(2)}) copy-start(f32[1024]{0:T(1024)} %param.7) | copy-start | bytes 12292
